TPU v7x, 64 devices: a 2x2x8 block of a 4x4x8 slice. The times are simulated.
64 devices in a mesh: dp: 4 (over x, y), tp: 16 (over z, core).
Axes of the slice: x: 2, y: 2, z: 8, core: 2. Of those that a mesh axis runs over, the one named last changes fastest.
The devices are a block of a 4x4x8 slice.
Arguments:
- x: bfloat16 [256, 2048], P('dp'), parts along dimension 0
- k_cache: bfloat16 [256, 2048, 16, 128], P('dp', None, 'tp'), parts along dimension 0
- v_cache: bfloat16 [256, 2048, 16, 128], P('dp', None, 'tp'), parts along dimension 0
- gain_a: bfloat16 [2048], replicated
- wq: bfloat16 [2048, 2048], P(None, 'tp')
- wo: bfloat16 [2048, 2048], P('tp')
- gain_m: bfloat16 [2048], replicated
- w_gate: bfloat16 [2048, 8192], P(None, 'tp')
- w_up: bfloat16 [2048, 8192], P(None, 'tp')
- w_down: bfloat16 [8192, 2048], P('tp')
Outputs:
- output: bfloat16 [256, 2048], P('dp'), parts along dimension 0
There are 4 independent parts. A program takes and returns all parts, laid end to end along the dimension named above; an argument that names none is the same for every part.
All inputs are finite; a program needn't handle non-finite values.
Results may differ from a plain program's by a relative error of at most 0.017.
Values are sent between devices in bfloat16 or wider.
A program may use at most 768 MiB of HBM per device.

v0:
```python
import jax
import jax.numpy as jnp
from jax import lax
from jax.sharding import PartitionSpec as P

HEAD = 128
THETA = 10000


def normed(x, gain):
    wide = x.astype(jnp.float32)
    scale = lax.rsqrt(jnp.mean(wide * wide, -1, keepdims=True) + 1e-6)
    return (wide * scale * gain.astype(jnp.float32)).astype(jnp.bfloat16)


def turned(t, place, theta):
    half = t.shape[-1] // 2
    angle = place.astype(jnp.float32)[:, None] * theta ** (-jnp.arange(half, dtype=jnp.float32) / half)
    cos, sin = jnp.cos(angle)[:, None], jnp.sin(angle)[:, None]
    a, b = t[..., :half].astype(jnp.float32), t[..., half:].astype(jnp.float32)
    return jnp.concatenate([a * cos - b * sin, b * cos + a * sin], -1).astype(jnp.bfloat16)


def matmul(a, w):
    return jnp.dot(a, w, preferred_element_type=jnp.float32).astype(jnp.bfloat16)


def einsum(form, a, b):
    return jnp.einsum(form, a.astype(jnp.float32), b.astype(jnp.float32))


def seen_by(a, wq, k_cache, v_cache, head, theta):
    batch, cache, kv_heads = k_cache.shape[:3]
    place = jnp.full((batch,), cache - 1)
    q = turned(matmul(a, wq).reshape(batch, -1, head), place, theta).reshape(batch, kv_heads, -1, head)
    scores = einsum("bgsd,bugd->bgsu", q, k_cache) * head**-0.5
    weights = jax.nn.softmax(scores, -1).astype(jnp.bfloat16)
    return einsum("bgsu,bugd->bgsd", weights, v_cache).astype(jnp.bfloat16).reshape(batch, -1)


def hidden_of(b, w_gate, w_up):
    gate = jnp.dot(b, w_gate, preferred_element_type=jnp.float32)
    up = jnp.dot(b, w_up, preferred_element_type=jnp.float32)
    return (jax.nn.silu(gate) * up).astype(jnp.bfloat16)


def solution(mesh):
    def added(t, term):
        return (t.astype(jnp.float32) + lax.psum(term.astype(jnp.bfloat16), "tp").astype(jnp.float32)).astype(jnp.bfloat16)

    def step(x, k_cache, v_cache, gain_a, wq, wo, gain_m, w_gate, w_up, w_down):
        seen = seen_by(normed(x, gain_a), wq, k_cache, v_cache, HEAD, THETA)
        h = added(x, jnp.dot(seen, wo, preferred_element_type=jnp.float32))
        return added(h, jnp.dot(hidden_of(normed(h, gain_m), w_gate, w_up), w_down, preferred_element_type=jnp.float32))

    states, cache, columns, rows_of = P("dp", None), P("dp", None, "tp", None), P(None, "tp"), P("tp", None)
    return jax.shard_map(
        step,
        mesh=mesh,
        in_specs=(states, cache, cache, P(None), columns, rows_of, P(None), columns, columns, rows_of),
        out_specs=states,
        check_vma=False,
    )
```

profile of v0, /device:TPU:21, one launch (start us, length us, event | category | flops | bytes accessed | tf_op | source)
XLA Modules:
  0.0 267.0 jit_solution(2409529097625796639)
XLA Ops:
  6.5 0.0 copy-start
  6.6 0.8 convert_element_type.68
  7.4 1.1 fusion.6
  8.6 1.4 fusion.5
  10.0 0.1 fusion.37
  10.1 0.1 maximum_bitcast_fusion
  10.1 14.4 %fusion.2 = f32[64,1,2048]{2,1,0:T(1,128)S(1)} fusion(bf16[64,2048,1,128]{3,1,2,0:T(8,128)(2,1)} %param.11, bf16[64,128,1]{1,0,2:T(8,128)(2,1)S(1)} %maximum_bitcast_fusion), kind=kOutput, calls=%fused_computation.2 | convolution fusion | flops 33554432 | bytes 34095104 | tf_op jit(solution)/shard_map/bgsd,bugd->bgsu/dot_general | solution.py:29
  24.6 0.3 fusion.16
  24.9 0.3 fusion.15
  25.2 0.2 fusion.20
  25.4 0.0 copy-start.2
  25.4 0.0 copy-start.3
  25.5 0.0 copy-start.1
  25.5 12.9 %fusion = f32[64,1,128]{2,1,0:T(1,128)S(1)} fusion(bf16[64,2048,1,128]{3,1,2,0:T(8,128)(2,1)} %param.12, bf16[64,2048,1]{1,0,2:T(8,128)(2,1)S(1)} %fusion.20), kind=kOutput, calls=%fused_computation | convolution fusion | flops 33554432 | bytes 33849344 | tf_op jit(solution)/shard_map/bgsu,bugd->bgsd/dot_general | solution.py:29
  38.4 0.9 convolution_convert_fusion.1
  39.3 0.1 all-reduce.3.cloned.1.call-update
  39.4 0.1 all-reduce.5.cloned.1.call-start
  39.5 108.2 %all-reduce.3.cloned.1.call-done = bf16[64,2048]{1,0:T(8,128)(2,1)} async-done(((bf16[64,2048]{1,0:T(8,128)(2,1)}), bf16[64,2048]{1,0:T(8,128)(2,1)}) %all-reduce.3.cloned.1.call-update) | async-done | bytes 262160 | tf_op jit(solution)/shard_map/psum | solution.py:49
  147.7 1.1 fusion.10
  148.8 2.1 fusion.28
  151.0 3.3 %convolution_convert_fusion = bf16[64,2048]{1,0:T(8,128)(2,1)} fusion(bf16[512,2048]{1,0:T(8,128)(2,1)S(1)} %copy-done, bf16[2048,512]{1,0:T(8,128)(2,1)} %param.18, f32[64,512]{1,0:T(8,128)S(1)} %fusion.28, bf16[64,2048]{1,0:T(8,128)(2,1)S(1)} %get-tuple-element.6, f32[2048]{0:T(1024)S(1)} %convert_element_type.79, f32[64]{0:T(128)S(1)} %add_rsqrt_fusion), kind=kOutput, calls=%fused_computation.4 | convolution fusion | flops 269287424 | bytes 4858112 | tf_op jit(solution)/shard_map/dot_general | solution.py:54
  154.2 0.1 all-reduce.5.cloned.1.call-update
  154.3 104.1 %all-reduce.5.cloned.1.call-done = bf16[64,2048]{1,0:T(8,128)(2,1)} async-done(((bf16[64,2048]{1,0:T(8,128)(2,1)}), bf16[64,2048]{1,0:T(8,128)(2,1)}) %all-reduce.5.cloned.1.call-update) | async-done | bytes 262160 | tf_op jit(solution)/shard_map/psum | solution.py:49
  258.4 1.7 fusion.13
  (9 shorter events, 0.1 us)
Async XLA Ops:
  6.5 144.4 %copy-start = (bf16[512,2048]{1,0:T(8,128)(2,1)S(1)}, bf16[512,2048]{1,0:T(8,128)(2,1)}, u32[]{:S(2)}) copy-start(bf16[512,2048]{1,0:T(8,128)(2,1)} %param.19) | copy-start | bytes 6291460
  6.6 141.1 %all-reduce.3.cloned.1.call-start = ((), (), s32[]{:S(2)}) async-start(), calls=%async_computation | async-start | bytes 524288 | tf_op jit(solution)/shard_map/psum | solution.py:49
  25.4 13.0 %copy-start.2 = (bf16[128,2048]{1,0:T(8,128)(2,1)S(1)}, bf16[128,2048]{1,0:T(8,128)(2,1)}, u32[]{:S(2)}) copy-start(bf16[128,2048]{1,0:T(8,128)(2,1)} %param.15) | copy-start | bytes 1572868
  25.4 14.0 %copy-start.3 = (bf16[2048]{0:T(1024)(128)(2,1)S(1)}, bf16[2048]{0:T(1024)(128)(2,1)}, u32[]{:S(2)}) copy-start(bf16[2048]{0:T(1024)(128)(2,1)} %param.16) | copy-start | bytes 12292
  25.5 122.2 %copy-start.1 = (bf16[64,2048]{1,0:T(8,128)(2,1)S(1)}, bf16[64,2048]{1,0:T(8,128)(2,1)}, u32[]{:S(2)}) copy-start(bf16[64,2048]{1,0:T(8,128)(2,1)} %param.10) | copy-start | bytes 786436
  39.4 219.0 %all-reduce.5.cloned.1.call-start = ((), (), s32[]{:S(2)}) async-start(), calls=%async_computation.1 | async-start | bytes 524288 | tf_op jit(solution)/shard_map/psum | solution.py:49
Sparse Core Ops, SparseCore 0:
  39.5 108.1 all-reduce.2
  154.4 103.9 all-reduce.4
where the time goes:
time: 267 us
  waiting for transfers between devices  212 us (79%)
  matrix products  35.1 us (13%)
  between operations  13.5 us (5%)
  other arithmetic  5.85 us (2%)
    psum x2, waiting for transfers between devices, added(): lax.psum(term.astype(jnp.bfloat16), 'tp').astype(jnp.float32)  212 us
    dot_general x2, matrix products, einsum(): return jnp.einsum(form, a.astype(jnp.float32), b.astype(jnp.float32))  27.4 us
  transfers between devices with their start and end apart: 2, of which 2 were waited for; matrix products, arithmetic and copies ran while one was open for 0% of the time, Pallas kernels for 0%

commit v1 on v0

v1 whole, which is shorter than its diff:
```python
import functools

import jax
import jax.numpy as jnp
import numpy as np
from jax import lax
from jax.experimental import pallas as pl
from jax.experimental.pallas import tpu as pltpu
from jax.sharding import PartitionSpec as P

HEAD = 128
THETA = 10000
CHUNK = 16
SLOTS = 3
TILE = 256
EPS = 1e-6
MESH = pl.DeviceIdType.MESH
F32, BF16 = jnp.float32, jnp.bfloat16


def far_first(n):
    return sorted(range(1, n), key=lambda d: -min(d, n - d))


def kernel(n, x_hbm, k_hbm, v_hbm, ga_hbm, wq_hbm, wo_hbm, gm_hbm, wg_hbm, wu_hbm, wd_hbm, rot_hbm, out_ref,
           kbuf, vbuf, x_v, a_v, ga_v, gm_v, rot_v, wq_v, wo_v, wg_v, wu_v, wd_v, q_v, s_v, p_v, f_v, own_v, hown_v,
           t1, r1, hh, t2, r2, yy, ksem, vsem, wsem, send_sem, recv_sem):
    me = lax.axis_index("tp")
    rows, d_model = x_v.shape
    chunks = rows // CHUNK
    cache = kbuf.shape[2]
    pairs = CHUNK // 2
    width = d_model // n

    barrier = pltpu.get_barrier_semaphore()
    for d in range(1, n):
        pl.semaphore_signal(barrier, inc=1, device_id={"tp": lax.rem(me + d, n)}, device_id_type=MESH)

    small = [(x_hbm, x_v), (wq_hbm, wq_v), (ga_hbm, ga_v), (rot_hbm, rot_v), (wo_hbm, wo_v), (gm_hbm, gm_v),
             (wg_hbm, wg_v), (wu_hbm, wu_v), (wd_hbm, wd_v)]

    def load(i):
        return pltpu.make_async_copy(small[i][0], small[i][1], wsem.at[i])

    def kv(hbm, buf, sem, c, j):
        slot = lax.rem(c, SLOTS)
        return pltpu.make_async_copy(hbm.at[pl.ds(c * CHUNK + 2 * j, 2)], buf.at[slot, pl.ds(2 * j, 2)], sem.at[slot, j])

    def start_k(c):
        for j in range(pairs):
            kv(k_hbm, kbuf, ksem, c, j).start()

    def start_v(c):
        for j in range(pairs):
            kv(v_hbm, vbuf, vsem, c, j).start()

    for i in range(4):
        load(i).start()
    for c in range(min(SLOTS, chunks)):
        start_k(c)
        start_v(c)
        if c == 0:
            load(4).start()
            load(5).start()
        if c == 1:
            for i in range(6, 9):
                load(i).start()

    for i in range(4):
        load(i).wait()
    gain_a = ga_v[...].astype(F32)
    for c in range(chunks):
        wide = x_v[c * CHUNK:(c + 1) * CHUNK, :].astype(F32)
        scale = lax.rsqrt(jnp.mean(wide * wide, -1, keepdims=True) + EPS)
        a_v[c * CHUNK:(c + 1) * CHUNK, :] = (wide * scale * gain_a).astype(BF16)
    q = jnp.dot(a_v[...], wq_v[...], preferred_element_type=F32).astype(BF16).astype(F32)
    q_v[...] = (q * rot_v[0:1, :] + pltpu.roll(q, HEAD // 2, 1) * rot_v[1:2, :]).astype(BF16)

    row = lax.broadcasted_iota(jnp.int32, (CHUNK, HEAD), 0)

    def send_all(phase, c, source, target):
        for d in far_first(n):
            to = lax.rem(me + d, n)
            pltpu.make_async_remote_copy(
                src_ref=source(to, d), dst_ref=target(to, d), send_sem=send_sem.at[phase, c], recv_sem=recv_sem.at[phase, c],
                device_id={"tp": to}, device_id_type=MESH).start()

    def arrived(phase, c, ref):
        block = ref.at[c, pl.ds(0, n - 1)]
        pltpu.make_async_remote_copy(
            src_ref=block, dst_ref=block, send_sem=send_sem.at[phase, c], recv_sem=recv_sem.at[phase, c],
            device_id={"tp": me}, device_id_type=MESH).wait_recv()

    def sent(phase, c, ref):
        block = ref.at[c, pl.ds(0, n - 1)]
        pltpu.make_async_remote_copy(
            src_ref=block, dst_ref=block, send_sem=send_sem.at[phase, c], recv_sem=recv_sem.at[phase, c],
            device_id={"tp": me}, device_id_type=MESH).wait_send()

    def scatter(phase, c, term, t, r):
        for k in range(n):
            part = term[:, k * width:(k + 1) * width]
            f_v[k] = part
            t[c, k] = part.astype(BF16)
        own_v[phase // 2, c] = f_v[me]
        send_all(phase, c, lambda to, d: t.at[c, to], lambda to, d: r.at[c, d - 1])

    def gathered(phase, c, r):
        arrived(phase, c, r)
        total = own_v[phase // 2, c]
        for d in range(n - 1):
            total = total + r[c, d].astype(F32)
        return total

    def attention(c):
        slot = lax.rem(c, SLOTS)
        queries = q_v[pl.ds(pl.multiple_of(c * CHUNK, CHUNK), CHUNK), :].astype(F32)
        for j in range(pairs):
            kv(k_hbm, kbuf, ksem, c, j).wait()
            both = jnp.concatenate([jnp.where(row == 2 * j, queries, 0.0), jnp.where(row == 2 * j + 1, queries, 0.0)], -1).astype(BF16)
            for t in range(0, cache, TILE):
                keys = jnp.concatenate([kbuf[slot, 2 * j, t:t + TILE, :], kbuf[slot, 2 * j + 1, t:t + TILE, :]], -1)
                part = lax.dot_general(both, keys, (((1,), (1,)), ((), ())), preferred_element_type=F32)
                if j == 0:
                    s_v[:, t:t + TILE] = part
                else:
                    s_v[:, t:t + TILE] += part

        @pl.when(c + SLOTS < chunks)
        def _():
            start_k(c + SLOTS)

        scores = s_v[...] * HEAD**-0.5
        e = jnp.exp(scores - jnp.max(scores, -1, keepdims=True))
        p_v[...] = (e / jnp.sum(e, -1, keepdims=True)).astype(BF16)
        seen = jnp.zeros((CHUNK, HEAD), F32)
        for j in range(pairs):
            kv(v_hbm, vbuf, vsem, c, j).wait()
            values = jnp.concatenate([vbuf[slot, 2 * j], vbuf[slot, 2 * j + 1]], -1)
            both = jnp.dot(p_v[...], values, preferred_element_type=F32)
            seen = jnp.where(row == 2 * j, both[:, :HEAD], seen)
            seen = jnp.where(row == 2 * j + 1, both[:, HEAD:], seen)

        @pl.when(c + SLOTS < chunks)
        def _():
            start_v(c + SLOTS)

        @pl.when(c == 0)
        def _():
            load(4).wait()
            pl.semaphore_wait(barrier, n - 1)

        scatter(0, c, jnp.dot(seen.astype(BF16), wo_v[...], preferred_element_type=F32), t1, r1)

    def finish_h(c):
        mine = x_v[pl.ds(pl.multiple_of(c * CHUNK, CHUNK), CHUNK), pl.ds(pl.multiple_of(me * width, width), width)]
        h = (mine.astype(F32) + gathered(0, c, r1)).astype(BF16)
        hown_v[c] = h
        hh[c, me] = h
        send_all(1, c, lambda to, d: hh.at[c, me], lambda to, d: hh.at[c, me])

    def mlp(c):
        @pl.when(c == 0)
        def _():
            for i in range(5, 9):
                load(i).wait()

        arrived(1, c, hh)
        squares = jnp.zeros((CHUNK, width), F32)
        for k in range(n):
            wide = hh[c, k].astype(F32)
            squares = squares + wide * wide
        scale = lax.rsqrt(jnp.sum(squares, -1, keepdims=True) / d_model + EPS)
        b = jnp.concatenate(
            [(hh[c, k].astype(F32) * scale * gm_v[:, k * width:(k + 1) * width].astype(F32)).astype(BF16) for k in range(n)], -1)
        gate = jnp.dot(b, wg_v[...], preferred_element_type=F32)
        up = jnp.dot(b, wu_v[...], preferred_element_type=F32)
        hidden = (gate * jax.nn.sigmoid(gate) * up).astype(BF16)
        scatter(2, c, jnp.dot(hidden, wd_v[...], preferred_element_type=F32), t2, r2)

    def finish_y(c):
        yy[c, me] = (hown_v[c].astype(F32) + gathered(2, c, r2)).astype(BF16)
        send_all(3, c, lambda to, d: yy.at[c, me], lambda to, d: yy.at[c, me])

    def step(s, carry):
        for lag, stage in enumerate((attention, finish_h, mlp, finish_y)):
            @pl.when((s >= lag) & (s < chunks + lag))
            def _(stage=stage, lag=lag):
                stage(s - lag)

        return carry

    lax.fori_loop(0, chunks + 3, step, 0)

    for c in range(chunks):
        arrived(3, c, yy)
        for k in range(n):
            out_ref[c * CHUNK:(c + 1) * CHUNK, k * width:(k + 1) * width] = yy[c, k]
    for c in range(chunks):
        for phase, ref in enumerate((t1, hh, t2, yy)):
            sent(phase, c, ref)


def rotation(place):
    half = HEAD // 2
    angle = np.float64(place) * float(THETA) ** (-np.arange(half) / half)
    cos, sin = np.cos(angle), np.sin(angle)
    table = np.zeros((8, HEAD), np.float32)
    table[0], table[1] = np.concatenate([cos, cos]), np.concatenate([-sin, sin])
    return table


def solution(mesh):
    n = mesh.shape["tp"]

    def step(x, k_cache, v_cache, gain_a, wq, wo, gain_m, w_gate, w_up, w_down):
        rows, d_model = x.shape
        cache = k_cache.shape[1]
        chunks, hidden, width = rows // CHUNK, w_gate.shape[1], d_model // n
        anywhere = pl.BlockSpec(memory_space=pl.ANY)
        tiles = pltpu.VMEM((chunks, n, CHUNK, width), BF16)
        arrivals = pltpu.VMEM((chunks, n - 1, CHUNK, width), BF16)
        dma = pltpu.SemaphoreType.DMA
        return pl.pallas_call(
            functools.partial(kernel, n),
            out_shape=jax.ShapeDtypeStruct((rows, d_model), BF16),
            in_specs=[anywhere] * 11,
            out_specs=pl.BlockSpec(memory_space=pltpu.VMEM),
            scratch_shapes=[
                pltpu.VMEM((SLOTS, CHUNK, cache, HEAD), BF16),
                pltpu.VMEM((SLOTS, CHUNK, cache, HEAD), BF16),
                pltpu.VMEM((rows, d_model), BF16),
                pltpu.VMEM((rows, d_model), BF16),
                pltpu.VMEM((1, d_model), BF16),
                pltpu.VMEM((1, d_model), BF16),
                pltpu.VMEM((8, HEAD), F32),
                pltpu.VMEM(wq.shape, BF16),
                pltpu.VMEM(wo.shape, BF16),
                pltpu.VMEM((d_model, hidden), BF16),
                pltpu.VMEM((d_model, hidden), BF16),
                pltpu.VMEM((hidden, d_model), BF16),
                pltpu.VMEM((rows, HEAD), BF16),
                pltpu.VMEM((CHUNK, cache), F32),
                pltpu.VMEM((CHUNK, cache), BF16),
                pltpu.VMEM((n, CHUNK, width), F32),
                pltpu.VMEM((2, chunks, CHUNK, width), F32),
                pltpu.VMEM((chunks, CHUNK, width), BF16),
                tiles, arrivals, tiles, tiles, arrivals, tiles,
                dma((SLOTS, CHUNK // 2)), dma((SLOTS, CHUNK // 2)), dma((9,)), dma((4, chunks)), dma((4, chunks)),
            ],
            compiler_params=pltpu.CompilerParams(collective_id=0, has_side_effects=True, vmem_limit_bytes=67043328),
        )(x, k_cache.reshape(rows, cache, HEAD), v_cache.reshape(rows, cache, HEAD), gain_a.reshape(1, -1), wq, wo,
          gain_m.reshape(1, -1), w_gate, w_up, w_down, jnp.asarray(rotation(cache - 1)))

    states, cache, columns, rows_of = P("dp", None), P("dp", None, "tp", None), P(None, "tp"), P("tp", None)
    return jax.shard_map(
        step,
        mesh=mesh,
        in_specs=(states, cache, cache, P(None), columns, rows_of, P(None), columns, columns, rows_of),
        out_specs=states,
        check_vma=False,
    )
```

time: 267 us -> 72.2 us (0.27)
  waiting for transfers between devices: 212 us -> 0 us
  Pallas kernels: 0 us -> 67.8 us
  matrix products: 35.1 us -> 0 us
  between operations: 13.5 us -> 0.01 us
  other arithmetic: 5.85 us -> 0 us
  local copies, waits for them, and re-layouts: 0.02 us -> 4.24 us
    psum x2 -> x0, waiting for transfers between devices: 212 us -> none  [added(): lax.psum(term.astype(jnp.bfloat16), 'tp').astype(jnp.float32)]
    pallas_call x0 -> x1, Pallas kernels: none -> 67.8 us  [step(): pl.pallas_call(functools.partial(kernel, n), out_shape=jax.ShapeDtypeStru...]
    dot_general x6 -> x0, matrix products: 35.1 us -> none  [the longest x2 27.4 us: einsum(): return jnp.einsum(form, a.astype(jnp.float32), b.astype(jnp.float32))]
    convert_element_type x4 -> x0, other arithmetic: 2.78 us -> none  [the longest x1 1.71 us: added(): (t.astype(jnp.float32) + lax.psum(term.astype(jnp.bfloat16), 'tp').astype...]
  transfers between devices with their start and end apart: 2 -> 0, of which waited for: 2 -> 0; matrix products, arithmetic and copies ran while one was open for 0% -> 0% of each run, Pallas kernels for 0% -> 0%
where the time goes in v1:
time: 72.2 us; the launch traced here: 72 us
  Pallas kernels  67.8 us (94%)
  local copies, waits for them, and re-layouts  4.24 us (6%)
    pallas_call x1, Pallas kernels, step(): pl.pallas_call(functools.partial(kernel, n), out_shape=jax.ShapeDtypeStru...  67.8 us
    unnamed x1, local copies, waits for them, and re-layouts  1.67 us

profile of v1, /device:TPU:21, one launch (start us, length us, event | category | flops | bytes accessed | tf_op | source)
XLA Modules:
  0.0 72.0 jit_solution(2680968502684583725)
XLA Ops:
  0.0 1.3 %reshape.14.ga_hbm = bf16[1,2048]{1,0:T(2,128)(2,1)} reshape(bf16[2048]{0:T(1024)(128)(2,1)} %param.14) | data formatting | bytes 8192 | tf_op jit(solution)/shard_map/reshape | solution.py:252
  1.3 1.3 %reshape.15.gm_hbm = bf16[1,2048]{1,0:T(2,128)(2,1)} reshape(bf16[2048]{0:T(1024)(128)(2,1)} %param.17) | data formatting | bytes 8192 | tf_op jit(solution)/shard_map/reshape | solution.py:253
  2.6 67.8 %shard_map.109 = bf16[64,2048]{1,0:T(8,128)(2,1)} custom-call(bf16[64,2048]{1,0:T(8,128)(2,1)} %x_hbm.1, bf16[64,2048,128]{2,1,0:T(8,128)(2,1)} %bitcast.2, bf16[64,2048,128]{2,1,0:T(8,128)(2,1)} %bitcast.3, bf16[1,2048]{1,0:T(2,128)(2,1)} %reshape.14.ga_hbm, bf16[2048,128]{1,0:T(8,128)(2,1)} %wq_hbm.1, bf16[128,2048]{1,0:T(8,128)(2,1)} %wo_hbm.1, ...), custom_call_target="tpu_custom_call" | custom-call | tf_op jit(solution)/shard_map/pallas_call | solution.py:224
  70.4 1.7 %copy.13 = bf16[64,2048]{1,0:T(8,128)(2,1)} copy(bf16[64,2048]{1,0:T(8,128)(2,1)} %shard_map.109) | data formatting | bytes 524288

commit v2 on v1

v2 whole, which is shorter than its diff:
```python
import functools

import jax
import jax.numpy as jnp
import numpy as np
from jax import lax
from jax.experimental import pallas as pl
from jax.experimental.pallas import tpu as pltpu
from jax.sharding import PartitionSpec as P

HEAD = 128
THETA = 10000
CHUNK = 16
SLOTS = 2
AHEAD = 16
FIRST = 4
GROUP = 4
VMEM_LIMIT = 48 << 20
TILE = 256
EPS = 1e-6
MESH = pl.DeviceIdType.MESH
F32, BF16 = jnp.float32, jnp.bfloat16


def far_first(n):
    return sorted(range(1, n), key=lambda d: -min(d, n - d))


def kernel(n, x_hbm, k_hbm, v_hbm, ga_hbm, wq_hbm, wo_hbm, gm_hbm, wg_hbm, wu_hbm, wd_hbm, rot_hbm, out_ref,
           kbuf, vbuf, x_v, a_v, ga_v, gm_v, rot_v, wq_v, wo_v, wg_v, wu_v, wd_v, q_v, s_v, p_v, f_v, own_v, hown_v,
           t1, r1, hh, t2, r2, yy, ksem, vsem, wsem, send_sem, recv_sem):
    me = lax.axis_index("tp")
    rows, d_model = x_v.shape
    chunks = rows // CHUNK
    cache = kbuf.shape[2]
    pairs = CHUNK // 2
    width = d_model // n

    barrier = pltpu.get_barrier_semaphore()
    for d in range(1, n):
        pl.semaphore_signal(barrier, inc=1, device_id={"tp": lax.rem(me + d, n)}, device_id_type=MESH)

    small = [(x_hbm, x_v), (wq_hbm, wq_v), (ga_hbm, ga_v), (rot_hbm, rot_v), (wo_hbm, wo_v), (gm_hbm, gm_v),
             (wg_hbm, wg_v), (wu_hbm, wu_v), (wd_hbm, wd_v)]

    def load(i):
        return pltpu.make_async_copy(small[i][0], small[i][1], wsem.at[i])

    def kv(hbm, buf, sem, c, j):
        slot = lax.rem(c, SLOTS)
        return pltpu.make_async_copy(hbm.at[pl.ds(c * CHUNK + 2 * j, 2)], buf.at[slot, pl.ds(2 * j, 2)], sem.at[slot, j])

    def item(c, i):
        c, i = c + i // (2 * pairs), i % (2 * pairs)
        return kv(k_hbm, kbuf, ksem, c, i) if i < pairs else kv(v_hbm, vbuf, vsem, c, i - pairs)

    def refill(c, i):
        ramp = 2 * i + pairs + 1 <= i + AHEAD

        @pl.when(c == 0)
        def _():
            for m in (2 * i + pairs, 2 * i + pairs + 1) if ramp else (i + AHEAD,):
                item(0, m).start()

        @pl.when((c > 0) & (c + (i + AHEAD) // (2 * pairs) < chunks))
        def _():
            item(c, i + AHEAD).start()

    for i in range(4):
        load(i).start()
    for i in range(FIRST):
        item(0, i).start()

    with jax.named_scope("wait_x"):
        for i in (0, 2):
            load(i).wait()
    for c in range(chunks):
        wide = x_v[c * CHUNK:(c + 1) * CHUNK, :].astype(F32)
        scale = lax.rsqrt(jnp.mean(wide * wide, -1, keepdims=True) + EPS)
        for k in range(n):
            block = pl.ds(k * width, width)
            a_v[c * CHUNK:(c + 1) * CHUNK, block] = (wide[:, k * width:(k + 1) * width] * scale * ga_v[k:k + 1, :].astype(F32)).astype(BF16)
    with jax.named_scope("wait_wq"):
        for i in (1, 3):
            load(i).wait()
    load(4).start()
    for i in range(FIRST, pairs):
        item(0, i).start()
    q = jnp.dot(a_v[...], wq_v[...], preferred_element_type=F32).astype(BF16).astype(F32)
    q_v[...] = (q * rot_v[0:1, :] + pltpu.roll(q, HEAD // 2, 1) * rot_v[1:2, :]).astype(BF16)

    row = lax.broadcasted_iota(jnp.int32, (CHUNK, HEAD), 0)

    def send_all(phase, c, source, target):
        for d in far_first(n):
            to = lax.rem(me + d, n)
            pltpu.make_async_remote_copy(
                src_ref=source(to, d), dst_ref=target(to, d), send_sem=send_sem.at[phase, c], recv_sem=recv_sem.at[phase, c],
                device_id={"tp": to}, device_id_type=MESH).start()

    def arrived(phase, c, ref):
        block = ref.at[c, pl.ds(0, n - 1)]
        pltpu.make_async_remote_copy(
            src_ref=block, dst_ref=block, send_sem=send_sem.at[phase, c], recv_sem=recv_sem.at[phase, c],
            device_id={"tp": me}, device_id_type=MESH).wait_recv()

    def sent(phase, c, ref):
        block = ref.at[c, pl.ds(0, n - 1)]
        pltpu.make_async_remote_copy(
            src_ref=block, dst_ref=block, send_sem=send_sem.at[phase, c], recv_sem=recv_sem.at[phase, c],
            device_id={"tp": me}, device_id_type=MESH).wait_send()

    def split(phase, c, term, t):
        for k in range(n):
            part = term[:, k * width:(k + 1) * width]
            f_v[k] = part
            t[c, k] = part.astype(BF16)
        own_v[phase // 2, c] = f_v[me]

    def scatter(phase, c, t, r):
        send_all(phase, c, lambda to, d: t.at[c, to], lambda to, d: r.at[c, d - 1])

    def gathered(phase, c, r):
        with jax.named_scope("wait_terms"):
            arrived(phase, c, r)
        total = own_v[phase // 2, c]
        for d in range(n - 1):
            total = total + r[c, d].astype(F32)
        return total

    def attention(c):
        slot = lax.rem(c, SLOTS)
        queries = q_v[pl.ds(pl.multiple_of(c * CHUNK, CHUNK), CHUNK), :].astype(F32)
        for j in range(pairs):
            with jax.named_scope("wait_k"):
                kv(k_hbm, kbuf, ksem, c, j).wait()
            refill(c, j)
            with jax.named_scope("scores"):
                both = jnp.concatenate([jnp.where(row == 2 * j, queries, 0.0), jnp.where(row == 2 * j + 1, queries, 0.0)], -1).astype(BF16)
                for t in range(0, cache, TILE):
                    keys = jnp.concatenate([kbuf[slot, 2 * j, t:t + TILE, :], kbuf[slot, 2 * j + 1, t:t + TILE, :]], -1)
                    part = lax.dot_general(both, keys, (((1,), (1,)), ((), ())), preferred_element_type=F32)
                    if j == 0:
                        s_v[:, t:t + TILE] = part
                    else:
                        s_v[:, t:t + TILE] += part

        @pl.when(c == 0)
        def _():
            load(4).wait()
            with jax.named_scope("barrier"):
                pl.semaphore_wait(barrier, n - 1)

        @pl.when(c >= 2)
        def _():
            finish_h(c - 2)

        with jax.named_scope("softmax"):
            scores = s_v[...] * HEAD**-0.5
            e = jnp.exp(scores - jnp.max(scores, -1, keepdims=True))
            p_v[...] = (e / jnp.sum(e, -1, keepdims=True)).astype(BF16)
        seen = jnp.zeros((CHUNK, HEAD), F32)
        for j in range(0, pairs, GROUP):
            with jax.named_scope("wait_v"):
                for i in range(j, j + GROUP):
                    kv(v_hbm, vbuf, vsem, c, i).wait()
            for i in range(j, j + GROUP):
                refill(c, pairs + i)
            if j + GROUP == pairs:
                @pl.when(c == chunks - 1)
                def _():
                    for i in range(5, 9):
                        load(i).start()

            with jax.named_scope("values"):
                values = jnp.concatenate([vbuf[slot, 2 * j + i] for i in range(2 * GROUP)], -1)
                each = jnp.dot(p_v[...], values, preferred_element_type=F32)
                for i in range(2 * GROUP):
                    seen = jnp.where(row == 2 * j + i, each[:, i * HEAD:(i + 1) * HEAD], seen)

        with jax.named_scope("wo"):
            split(0, c, jnp.dot(seen.astype(BF16), wo_v[...], preferred_element_type=F32), t1)
            scatter(0, c, t1, r1)

    def finish_h(c):
        mine = x_v[pl.ds(pl.multiple_of(c * CHUNK, CHUNK), CHUNK), pl.ds(pl.multiple_of(me * width, width), width)]
        h = (mine.astype(F32) + gathered(0, c, r1)).astype(BF16)
        hown_v[c] = h
        hh[c, me] = h
        send_all(1, c, lambda to, d: hh.at[c, me], lambda to, d: hh.at[c, me])

    def normed(c):
        with jax.named_scope("wait_h"):
            arrived(1, c, hh)
        squares = jnp.zeros((CHUNK, width), F32)
        for k in range(n):
            wide = hh[c, k].astype(F32)
            squares = squares + wide * wide
        scale = lax.rsqrt(jnp.sum(squares, -1, keepdims=True) / d_model + EPS)
        return jnp.concatenate([(hh[c, k].astype(F32) * scale * gm_v[k:k + 1, :].astype(F32)).astype(BF16) for k in range(n)], -1)

    def mlp(*which):
        b = jnp.concatenate([normed(c) for c in which], 0)
        with jax.named_scope("mlp"):
            gate = jnp.dot(b, wg_v[...], preferred_element_type=F32)
            up = jnp.dot(b, wu_v[...], preferred_element_type=F32)
            hidden = (gate * jax.nn.sigmoid(gate) * up).astype(BF16)
            term = jnp.dot(hidden, wd_v[...], preferred_element_type=F32)
            for i, c in enumerate(which):
                split(2, c, term[i * CHUNK:(i + 1) * CHUNK], t2)

    def finish_y(c):
        yy[c, me] = (hown_v[c].astype(F32) + gathered(2, c, r2)).astype(BF16)
        send_all(3, c, lambda to, d: yy.at[c, me], lambda to, d: yy.at[c, me])

    def step(c, carry):
        attention(c)
        return carry

    lax.fori_loop(0, chunks, step, 0)

    *early, late, last = range(chunks)
    finish_h(late)
    with jax.named_scope("wait_w"):
        for i in range(5, 9):
            load(i).wait()
    mlp(*early)
    finish_h(last)
    for c in early:
        scatter(2, c, t2, r2)
    mlp(late)
    scatter(2, late, t2, r2)
    mlp(last)
    scatter(2, last, t2, r2)
    for c in (*early, late, last):
        finish_y(c)

    for c in range(chunks):
        if c == last:
            for i in range(chunks):
                for phase, ref in enumerate((t1, hh, t2)):
                    sent(phase, i, ref)
                if i != last:
                    sent(3, i, yy)
        with jax.named_scope("wait_y"):
            arrived(3, c, yy)
        for k in range(n):
            out_ref[c * CHUNK:(c + 1) * CHUNK, k * width:(k + 1) * width] = yy[c, k]
    sent(3, last, yy)


def rotation(place):
    half = HEAD // 2
    angle = np.float64(place) * float(THETA) ** (-np.arange(half) / half)
    cos, sin = np.cos(angle), np.sin(angle)
    table = np.zeros((8, HEAD), np.float32)
    table[0], table[1] = np.concatenate([cos, cos]), np.concatenate([-sin, sin])
    return table


def solution(mesh):
    n = mesh.shape["tp"]

    def step(x, k_cache, v_cache, gain_a, wq, wo, gain_m, w_gate, w_up, w_down):
        rows, d_model = x.shape
        cache = k_cache.shape[1]
        chunks, hidden, width = rows // CHUNK, w_gate.shape[1], d_model // n
        anywhere = pl.BlockSpec(memory_space=pltpu.HBM)
        tiles = pltpu.VMEM((chunks, n, CHUNK, width), BF16)
        arrivals = pltpu.VMEM((chunks, n - 1, CHUNK, width), BF16)
        dma = pltpu.SemaphoreType.DMA
        return pl.pallas_call(
            functools.partial(kernel, n),
            out_shape=jax.ShapeDtypeStruct((rows, d_model), BF16),
            in_specs=[anywhere] * 11,
            out_specs=pl.BlockSpec(memory_space=pltpu.VMEM),
            scratch_shapes=[
                pltpu.VMEM((SLOTS, CHUNK, cache, HEAD), BF16),
                pltpu.VMEM((SLOTS, CHUNK, cache, HEAD), BF16),
                pltpu.VMEM((rows, d_model), BF16),
                pltpu.VMEM((rows, d_model), BF16),
                pltpu.VMEM((n, width), BF16),
                pltpu.VMEM((n, width), BF16),
                pltpu.VMEM((8, HEAD), F32),
                pltpu.VMEM(wq.shape, BF16),
                pltpu.VMEM(wo.shape, BF16),
                pltpu.VMEM((d_model, hidden), BF16),
                pltpu.VMEM((d_model, hidden), BF16),
                pltpu.VMEM((hidden, d_model), BF16),
                pltpu.VMEM((rows, HEAD), BF16),
                pltpu.VMEM((CHUNK, cache), F32),
                pltpu.VMEM((CHUNK, cache), BF16),
                pltpu.VMEM((n, CHUNK, width), F32),
                pltpu.VMEM((2, chunks, CHUNK, width), F32),
                pltpu.VMEM((chunks, CHUNK, width), BF16),
                tiles, arrivals, tiles, tiles, arrivals, tiles,
                dma((SLOTS, CHUNK // 2)), dma((SLOTS, CHUNK // 2)), dma((9,)), dma((4, chunks)), dma((4, chunks)),
            ],
            compiler_params=pltpu.CompilerParams(collective_id=0, has_side_effects=True, vmem_limit_bytes=VMEM_LIMIT),
        )(*(pltpu.with_memory_space_constraint(a, pltpu.HBM) for a in (
            x, k_cache.reshape(rows, cache, HEAD), v_cache.reshape(rows, cache, HEAD), gain_a.reshape(n, width), wq, wo,
            gain_m.reshape(n, width), w_gate, w_up, w_down, jnp.asarray(rotation(cache - 1)))))

    states, cache, columns, rows_of = P("dp", None), P("dp", None, "tp", None), P(None, "tp"), P("tp", None)
    return jax.shard_map(
        step,
        mesh=mesh,
        in_specs=(states, cache, cache, P(None), columns, rows_of, P(None), columns, columns, rows_of),
        out_specs=states,
        check_vma=False,
    )
```

time: 72.2 us -> 51.3 us (0.71)
  Pallas kernels: 67.8 us -> 50.5 us
  local copies, waits for them, and re-layouts: 4.24 us -> 0.71 us
    pallas_call x1, Pallas kernels: 67.8 us -> 50.5 us  [step(): pl.pallas_call(functools.partial(kernel, n), out_shape=jax.ShapeDtypeStru...]
    reshape x2 -> x0, local copies, waits for them, and re-layouts: 2.57 us -> none  [the longest x1 1.29 us: step(): gain_a.reshape(1, -1)]
    unnamed x1, local copies, waits for them, and re-layouts: 1.67 us -> 0.71 us
where the time goes in v2:
time: 51.3 us; the launch traced here: 51.2 us
  Pallas kernels  50.5 us (98%)
  local copies, waits for them, and re-layouts  0.71 us (1%)
    pallas_call x1, Pallas kernels, step(): pl.pallas_call(functools.partial(kernel, n), out_shape=jax.ShapeDtypeStru...  50.5 us

profile of v2, /device:TPU:21, one launch (start us, length us, event | category | flops | bytes accessed | tf_op | source)
XLA Modules:
  0.0 51.2 jit_solution(16241854845255797625)
XLA Ops:
  0.0 50.5 %shard_map.109 = bf16[64,2048]{1,0:T(8,128)(2,1)S(1)} custom-call(bf16[64,2048]{1,0:T(8,128)(2,1)} %x_hbm.1, bf16[64,2048,128]{2,1,0:T(8,128)(2,1)} %bitcast.4, bf16[64,2048,128]{2,1,0:T(8,128)(2,1)} %bitcast.5, bf16[16,128]{1,0:T(8,128)(2,1)} %bitcast.6, bf16[2048,128]{1,0:T(8,128)(2,1)} %wq_hbm.1, bf16[128,2048]{1,0:T(8,128)(2,1)} %wo_hbm.1, ...), custom_call_target="tpu_custom_call" | custom-call | tf_op jit(solution)/shard_map/pallas_call | solution.py:272
  50.5 0.7 %copy.13 = bf16[64,2048]{1,0:T(8,128)(2,1)} copy(bf16[64,2048]{1,0:T(8,128)(2,1)S(1)} %shard_map.109) | data formatting | bytes 524288

commit v3 on v2

--- a/solution.py
+++ b/solution.py
@@ -22,19 +22,29 @@
 F32, BF16 = jnp.float32, jnp.bfloat16
 
 
+def paired(early, late, last):
+    return [(1, late), (2, late), (3, late), *((phase, c) for phase in (2, 3) for c in early)]
+
+
 def far_first(n):
     return sorted(range(1, n), key=lambda d: -min(d, n - d))
 
 
 def kernel(n, x_hbm, k_hbm, v_hbm, ga_hbm, wq_hbm, wo_hbm, gm_hbm, wg_hbm, wu_hbm, wd_hbm, rot_hbm, out_ref,
            kbuf, vbuf, x_v, a_v, ga_v, gm_v, rot_v, wq_v, wo_v, wg_v, wu_v, wd_v, q_v, s_v, p_v, f_v, own_v, hown_v,
-           t1, r1, hh, t2, r2, yy, ksem, vsem, wsem, send_sem, recv_sem):
+           t1, r1, hh, t2, r2, yy, rx, ksem, vsem, wsem, send_sem, recv_sem, near_send, near_recv):
     me = lax.axis_index("tp")
     rows, d_model = x_v.shape
     chunks = rows // CHUNK
     cache = kbuf.shape[2]
     pairs = CHUNK // 2
     width = d_model // n
+    *early, late, last = range(chunks)
+    chips = n // 2
+    chip, core = lax.div(me, 2), lax.rem(me, 2)
+
+    def by_chip(phase, c):
+        return isinstance(c, int) and (phase, c) in paired(early, late, last)
 
     barrier = pltpu.get_barrier_semaphore()
     for d in range(1, n):
@@ -91,42 +101,74 @@
 
     row = lax.broadcasted_iota(jnp.int32, (CHUNK, HEAD), 0)
 
+    def remote(source, target, send, recv, to):
+        return pltpu.make_async_remote_copy(
+            src_ref=source, dst_ref=target, send_sem=send, recv_sem=recv, device_id={"tp": to}, device_id_type=MESH)
+
     def send_all(phase, c, source, target):
-        for d in far_first(n):
-            to = lax.rem(me + d, n)
-            pltpu.make_async_remote_copy(
-                src_ref=source(to, d), dst_ref=target(to, d), send_sem=send_sem.at[phase, c], recv_sem=recv_sem.at[phase, c],
-                device_id={"tp": to}, device_id_type=MESH).start()
-
-    def arrived(phase, c, ref):
-        block = ref.at[c, pl.ds(0, n - 1)]
-        pltpu.make_async_remote_copy(
-            src_ref=block, dst_ref=block, send_sem=send_sem.at[phase, c], recv_sem=recv_sem.at[phase, c],
-            device_id={"tp": me}, device_id_type=MESH).wait_recv()
-
-    def sent(phase, c, ref):
-        block = ref.at[c, pl.ds(0, n - 1)]
-        pltpu.make_async_remote_copy(
-            src_ref=block, dst_ref=block, send_sem=send_sem.at[phase, c], recv_sem=recv_sem.at[phase, c],
-            device_id={"tp": me}, device_id_type=MESH).wait_send()
+        if by_chip(phase, c):
+            for d in far_first(chips):
+                there = lax.rem(chip + d, chips)
+                remote(source(core, there), target(d), send_sem.at[phase, c], recv_sem.at[phase, c], 2 * there + core).start()
+        else:
+            for d in far_first(n):
+                to = lax.rem(me + d, n)
+                remote(source(lax.rem(to, 2), lax.div(to, 2)), target(d), send_sem.at[phase, c], recv_sem.at[phase, c], to).start()
+
+    def tiles(phase, c):
+        return r1.at[0, pl.ds(0, (chips if by_chip(phase, c) else n) - 1)]
+
+    def arrived(phase, c):
+        remote(tiles(phase, c), tiles(phase, c), send_sem.at[phase, c], recv_sem.at[phase, c], me).wait_recv()
+
+    def near(phase, c, source, target):
+        return remote(source, target, near_send.at[phase, c], near_recv.at[phase, c], me + 1 - 2 * core)
+
+    def sent(phase, c):
+        remote(tiles(phase, c), tiles(phase, c), send_sem.at[phase, c], recv_sem.at[phase, c], me).wait_send()
+        if by_chip(phase, c):
+            near(phase, c, rx.at[0], rx.at[0]).wait_send()
 
     def split(phase, c, term, t):
         for k in range(n):
             part = term[:, k * width:(k + 1) * width]
-            f_v[k] = part
-            t[c, k] = part.astype(BF16)
-        own_v[phase // 2, c] = f_v[me]
+            f_v[c, k % 2, k // 2] = part
+            t[c, k % 2, k // 2] = part.astype(BF16)
+        if by_chip(phase, c):
+            near(phase, c, t.at[c, 1 - core], rx.at[c]).start()
 
     def scatter(phase, c, t, r):
-        send_all(phase, c, lambda to, d: t.at[c, to], lambda to, d: r.at[c, d - 1])
+        if by_chip(phase, c):
+            with jax.named_scope("wait_near"):
+                near(phase, c, rx.at[c], rx.at[c]).wait_recv()
+            for there in range(chips):
+                part = f_v[c, core, there] + rx[c, there].astype(F32)
+                f_v[c, core, there] = part
+                t[c, core, there] = part.astype(BF16)
+        own_v[phase // 2, c] = f_v[c, core, chip]
+        send_all(phase, c, lambda i, there: t.at[c, i, there], lambda d: r.at[c, d - 1])
 
     def gathered(phase, c, r):
         with jax.named_scope("wait_terms"):
-            arrived(phase, c, r)
+            arrived(phase, c)
         total = own_v[phase // 2, c]
-        for d in range(n - 1):
+        for d in range((chips if by_chip(phase, c) else n) - 1):
             total = total + r[c, d].astype(F32)
         return total
+
+    def spread(phase, c, ref):
+        send_all(phase, c, lambda i, there: ref.at[c, core, chip], lambda d: ref.at[c, core, chip])
+
+    def relay(phase, c, ref):
+        with jax.named_scope("wait_far"):
+            arrived(phase, c)
+        near(phase, c, ref.at[c, core], ref.at[c, core]).start()
+
+    def complete(phase, c):
+        if by_chip(phase, c):
+            near(phase, c, rx.at[0], rx.at[0]).wait_recv()
+        else:
+            arrived(phase, c)
 
     def attention(c):
         slot = lax.rem(c, SLOTS)
@@ -186,18 +228,18 @@
         mine = x_v[pl.ds(pl.multiple_of(c * CHUNK, CHUNK), CHUNK), pl.ds(pl.multiple_of(me * width, width), width)]
         h = (mine.astype(F32) + gathered(0, c, r1)).astype(BF16)
         hown_v[c] = h
-        hh[c, me] = h
-        send_all(1, c, lambda to, d: hh.at[c, me], lambda to, d: hh.at[c, me])
+        hh[c, core, chip] = h
+        spread(1, c, hh)
 
     def normed(c):
         with jax.named_scope("wait_h"):
-            arrived(1, c, hh)
+            complete(1, c)
         squares = jnp.zeros((CHUNK, width), F32)
         for k in range(n):
-            wide = hh[c, k].astype(F32)
+            wide = hh[c, k % 2, k // 2].astype(F32)
             squares = squares + wide * wide
         scale = lax.rsqrt(jnp.sum(squares, -1, keepdims=True) / d_model + EPS)
-        return jnp.concatenate([(hh[c, k].astype(F32) * scale * gm_v[k:k + 1, :].astype(F32)).astype(BF16) for k in range(n)], -1)
+        return jnp.concatenate([(hh[c, k % 2, k // 2].astype(F32) * scale * gm_v[k:k + 1, :].astype(F32)).astype(BF16) for k in range(n)], -1)
 
     def mlp(*which):
         b = jnp.concatenate([normed(c) for c in which], 0)
@@ -210,8 +252,8 @@
                 split(2, c, term[i * CHUNK:(i + 1) * CHUNK], t2)
 
     def finish_y(c):
-        yy[c, me] = (hown_v[c].astype(F32) + gathered(2, c, r2)).astype(BF16)
-        send_all(3, c, lambda to, d: yy.at[c, me], lambda to, d: yy.at[c, me])
+        yy[c, core, chip] = (hown_v[c].astype(F32) + gathered(2, c, r2)).astype(BF16)
+        spread(3, c, yy)
 
     def step(c, carry):
         attention(c)
@@ -219,34 +261,34 @@
 
     lax.fori_loop(0, chunks, step, 0)
 
-    *early, late, last = range(chunks)
     finish_h(late)
     with jax.named_scope("wait_w"):
         for i in range(5, 9):
             load(i).wait()
     mlp(*early)
     finish_h(last)
-    for c in early:
+    if by_chip(1, late):
+        relay(1, late, hh)
+    mlp(late)
+    for c in (*early, late):
         scatter(2, c, t2, r2)
-    mlp(late)
-    scatter(2, late, t2, r2)
     mlp(last)
     scatter(2, last, t2, r2)
-    for c in (*early, late, last):
+    for c in range(chunks):
         finish_y(c)
-
+    for c in range(chunks):
+        if by_chip(3, c):
+            relay(3, c, yy)
     for c in range(chunks):
         if c == last:
             for i in range(chunks):
-                for phase, ref in enumerate((t1, hh, t2)):
-                    sent(phase, i, ref)
-                if i != last:
-                    sent(3, i, yy)
+                for phase in range(4 if i != last else 3):
+                    sent(phase, i)
         with jax.named_scope("wait_y"):
-            arrived(3, c, yy)
+            complete(3, c)
         for k in range(n):
-            out_ref[c * CHUNK:(c + 1) * CHUNK, k * width:(k + 1) * width] = yy[c, k]
-    sent(3, last, yy)
+            out_ref[c * CHUNK:(c + 1) * CHUNK, k * width:(k + 1) * width] = yy[c, k % 2, k // 2]
+    sent(3, last)
 
 
 def rotation(place):
@@ -266,7 +308,7 @@
         cache = k_cache.shape[1]
         chunks, hidden, width = rows // CHUNK, w_gate.shape[1], d_model // n
         anywhere = pl.BlockSpec(memory_space=pltpu.HBM)
-        tiles = pltpu.VMEM((chunks, n, CHUNK, width), BF16)
+        tiles = pltpu.VMEM((chunks, 2, n // 2, CHUNK, width), BF16)
         arrivals = pltpu.VMEM((chunks, n - 1, CHUNK, width), BF16)
         dma = pltpu.SemaphoreType.DMA
         return pl.pallas_call(
@@ -290,11 +332,11 @@
                 pltpu.VMEM((rows, HEAD), BF16),
                 pltpu.VMEM((CHUNK, cache), F32),
                 pltpu.VMEM((CHUNK, cache), BF16),
-                pltpu.VMEM((n, CHUNK, width), F32),
+                pltpu.VMEM((chunks, 2, n // 2, CHUNK, width), F32),
                 pltpu.VMEM((2, chunks, CHUNK, width), F32),
                 pltpu.VMEM((chunks, CHUNK, width), BF16),
-                tiles, arrivals, tiles, tiles, arrivals, tiles,
-                dma((SLOTS, CHUNK // 2)), dma((SLOTS, CHUNK // 2)), dma((9,)), dma((4, chunks)), dma((4, chunks)),
+                tiles, arrivals, tiles, tiles, arrivals, tiles, pltpu.VMEM((chunks, n // 2, CHUNK, width), BF16),
+                dma((SLOTS, CHUNK // 2)), dma((SLOTS, CHUNK // 2)), dma((9,)), *[dma((4, chunks))] * 4,
             ],
             compiler_params=pltpu.CompilerParams(collective_id=0, has_side_effects=True, vmem_limit_bytes=VMEM_LIMIT),
         )(*(pltpu.with_memory_space_constraint(a, pltpu.HBM) for a in (

time: 51.3 us -> 50.1 us (0.977)
  Pallas kernels: 50.5 us -> 49.3 us
    pallas_call x1, Pallas kernels: 50.5 us -> 49.3 us  [step(): pl.pallas_call(functools.partial(kernel, n), out_shape=jax.ShapeDtypeStru...]
where the time goes in v3:
time: 50.1 us; the launch traced here: 50 us
  Pallas kernels  49.3 us (98%)
  local copies, waits for them, and re-layouts  0.71 us (1%)
    pallas_call x1, Pallas kernels, step(): pl.pallas_call(functools.partial(kernel, n), out_shape=jax.ShapeDtypeStru...  49.3 us

profile of v3, /device:TPU:21, one launch (start us, length us, event | category | flops | bytes accessed | tf_op | source)
XLA Modules:
  0.0 50.0 jit_solution(17266101773155319394)
XLA Ops:
  0.0 49.3 %shard_map.109 = bf16[64,2048]{1,0:T(8,128)(2,1)S(1)} custom-call(bf16[64,2048]{1,0:T(8,128)(2,1)} %x_hbm.1, bf16[64,2048,128]{2,1,0:T(8,128)(2,1)} %bitcast.4, bf16[64,2048,128]{2,1,0:T(8,128)(2,1)} %bitcast.5, bf16[16,128]{1,0:T(8,128)(2,1)} %bitcast.6, bf16[2048,128]{1,0:T(8,128)(2,1)} %wq_hbm.1, bf16[128,2048]{1,0:T(8,128)(2,1)} %wo_hbm.1, ...), custom_call_target="tpu_custom_call" | custom-call | tf_op jit(solution)/shard_map/pallas_call | solution.py:314
  49.3 0.7 %copy.13 = bf16[64,2048]{1,0:T(8,128)(2,1)} copy(bf16[64,2048]{1,0:T(8,128)(2,1)S(1)} %shard_map.109) | data formatting | bytes 524288

commit v4 on v3

v4 whole, which is shorter than its diff:
```python
import functools

import jax
import jax.numpy as jnp
import numpy as np
from jax import lax
from jax.experimental import pallas as pl
from jax.experimental.pallas import tpu as pltpu
from jax.sharding import PartitionSpec as P

HEAD = 128
THETA = 10000
CHUNK = 16
HALF = CHUNK // 2
SLOTS = 2
AHEAD = CHUNK
FIRST = 4
KEYS = 2
GROUP = 4
VMEM_LIMIT = 48 << 20
TILE = 256
EPS = 1e-6
MESH = pl.DeviceIdType.MESH
F32, BF16 = jnp.float32, jnp.bfloat16


def paired(early, mid, late):
    return [(1, mid), *((phase, c) for phase in (2, 3) for c in (*early, mid, late))]


def far_first(n):
    return sorted(range(1, n), key=lambda d: -min(d, n - d))


def kernel(n, x_hbm, k_hbm, v_hbm, ga_hbm, wq_hbm, wo_hbm, gm_hbm, wg_hbm, wu_hbm, wd_hbm, rot_hbm, out_ref,
           kbuf, vbuf, x_v, a_v, ga_v, gm_v, rot_v, wq_v, wo_v, wg_v, wu_v, wd_v, q_v, s_v, p_v, f_v, own_v, hown_v,
           t1, r1, hh, t2, r2, yy, rx, t1h, r1h, hhh, t2h, r2h, yyh, rxh, ksem, vsem, wsem, send_sem, recv_sem, near_recv):
    t1, r1, hh, t2, r2, yy, rx = (t1, t1h), (r1, r1h), (hh, hhh), (t2, t2h), (r2, r2h), (yy, yyh), (rx, rxh)
    me = lax.axis_index("tp")
    rows, d_model = x_v.shape
    blocks = rows // CHUNK
    chunks = blocks + 1
    cache = kbuf.shape[2]
    pairs = CHUNK // 2
    width = d_model // n
    *early, mid, late, last = range(chunks)
    chips = n // 2
    chip, core = lax.div(me, 2), lax.rem(me, 2)

    def whole(c):
        return not isinstance(c, int) or c < late

    def size(c):
        return CHUNK if whole(c) else HALF

    def at(refs, c):
        return refs[0].at[c] if whole(c) else refs[1].at[c - late]

    def by_chip(phase, c):
        return isinstance(c, int) and (phase, c) in paired(early, mid, late)

    barrier = pltpu.get_barrier_semaphore()
    for d in range(1, n):
        pl.semaphore_signal(barrier, inc=1, device_id={"tp": lax.rem(me + d, n)}, device_id_type=MESH)

    small = [(x_hbm, x_v), (wq_hbm, wq_v), (ga_hbm, ga_v), (rot_hbm, rot_v), (wo_hbm, wo_v), (gm_hbm, gm_v),
             (wg_hbm, wg_v), (wu_hbm, wu_v), (wd_hbm, wd_v)]

    def load(i):
        return pltpu.make_async_copy(small[i][0], small[i][1], wsem.at[i])

    def kv(hbm, buf, sem, c, j, count=1, group=1):
        slot = lax.rem(c, SLOTS)
        return pltpu.make_async_copy(
            hbm.at[pl.ds(c * CHUNK + 2 * j, 2 * count)], buf.at[slot, pl.ds(2 * j, 2 * count)], sem.at[slot, j // group])

    def item(c, i, halves=False):
        if halves:
            i = i // pairs * (pairs // 2) + i % (pairs // 2) + i % pairs // (pairs // 2) * pairs
        return kv(k_hbm, kbuf, ksem, c, i, 1, KEYS) if i < pairs else kv(v_hbm, vbuf, vsem, c, i - pairs, 1, GROUP)

    def refill(c, i):
        if isinstance(c, int):
            return

        @pl.when(c == 0)
        def _():
            for m in (2 * i + pairs, 2 * i + pairs + 1) if 2 * i + pairs + 1 <= i + AHEAD else (i + AHEAD,):
                item(m // AHEAD, m % AHEAD).start()

        @pl.when((c > 0) & (c < blocks - 2))
        def _():
            item(c + 1, i).start()

        @pl.when(c == blocks - 2)
        def _():
            item(c + 1, i, True).start()

    for i in range(4):
        load(i).start()
    for i in range(FIRST):
        item(0, i).start()

    with jax.named_scope("wait_x"):
        for i in (0, 2):
            load(i).wait()
    for c in range(blocks):
        wide = x_v[c * CHUNK:(c + 1) * CHUNK, :].astype(F32)
        scale = lax.rsqrt(jnp.mean(wide * wide, -1, keepdims=True) + EPS)
        for k in range(n):
            block = pl.ds(k * width, width)
            a_v[c * CHUNK:(c + 1) * CHUNK, block] = (wide[:, k * width:(k + 1) * width] * scale * ga_v[k:k + 1, :].astype(F32)).astype(BF16)
    with jax.named_scope("wait_wq"):
        for i in (1, 3):
            load(i).wait()
    load(4).start()
    for i in range(FIRST, pairs):
        item(0, i).start()
    q = jnp.dot(a_v[...], wq_v[...], preferred_element_type=F32).astype(BF16).astype(F32)
    q_v[...] = (q * rot_v[0:1, :] + pltpu.roll(q, HEAD // 2, 1) * rot_v[1:2, :]).astype(BF16).astype(F32)

    row = lax.broadcasted_iota(jnp.int32, (CHUNK, HEAD), 0)

    def remote(source, target, send, recv, to):
        return pltpu.make_async_remote_copy(
            src_ref=source, dst_ref=target, send_sem=send, recv_sem=recv, device_id={"tp": to}, device_id_type=MESH)

    def send_all(phase, c, source, target):
        if by_chip(phase, c):
            for d in far_first(chips):
                there = lax.rem(chip + d, chips)
                remote(source(core, there), target(d), send_sem, recv_sem.at[phase, c], 2 * there + core).start()
        else:
            for d in far_first(n):
                to = lax.rem(me + d, n)
                remote(source(lax.rem(to, 2), lax.div(to, 2)), target(d), send_sem, recv_sem.at[phase, c], to).start()

    def tiles(phase, c):
        return r1[0 if whole(c) else 1].at[0, pl.ds(0, (chips if by_chip(phase, c) else n) - 1)]

    def arrived(phase, c):
        remote(tiles(phase, c), tiles(phase, c), send_sem, recv_sem.at[phase, c], me).wait_recv()

    def near(phase, c, source, target):
        return remote(source, target, send_sem, near_recv.at[paired(early, mid, late).index((phase, c))], me + 1 - 2 * core)

    def all_sent():
        count = sum(size(c) * (chips - 1 + chips if by_chip(phase, c) else n - 1) for phase in range(4) for c in range(chunks))
        ref = kbuf.at[0, pl.ds(0, count // TILE), pl.ds(0, TILE)]
        remote(ref, ref, send_sem, recv_sem.at[0, 0], me).wait_send()

    def split(phase, c, term, t):
        for k in range(n):
            part = term[:, k * width:(k + 1) * width]
            f_v[c, k % 2, k // 2, :size(c)] = part
            at(t, c)[k % 2, k // 2] = part.astype(BF16)
        if by_chip(phase, c):
            near(phase, c, at(t, c).at[1 - core], at(rx, c)).start()

    def scatter(phase, c, t, r):
        if by_chip(phase, c):
            with jax.named_scope("wait_near"):
                near(phase, c, at(rx, c), at(rx, c)).wait_recv()
            for there in range(chips):
                part = f_v[c, core, there, :size(c)] + at(rx, c)[there].astype(F32)
                f_v[c, core, there, :size(c)] = part
                at(t, c)[core, there] = part.astype(BF16)
        own_v[phase // 2, c, :size(c)] = f_v[c, core, chip, :size(c)]
        send_all(phase, c, lambda i, there: at(t, c).at[i, there], lambda d: at(r, c).at[d - 1])

    def gathered(phase, c, r):
        with jax.named_scope("wait_terms"):
            arrived(phase, c)
        total = own_v[phase // 2, c, :size(c)]
        for d in range((chips if by_chip(phase, c) else n) - 1):
            total = total + at(r, c)[d].astype(F32)
        return total

    def spread(phase, c, ref):
        send_all(phase, c, lambda i, there: at(ref, c).at[core, chip], lambda d: at(ref, c).at[core, chip])

    def relay(phase, c, ref):
        with jax.named_scope("wait_far"):
            arrived(phase, c)
        near(phase, c, at(ref, c).at[core], at(ref, c).at[core]).start()

    def complete(phase, c):
        if by_chip(phase, c):
            near(phase, c, at(rx, c), at(rx, c)).wait_recv()
        else:
            arrived(phase, c)

    def attention(c, half=None):
        slot = lax.rem(c, SLOTS)
        queries = q_v[pl.ds(pl.multiple_of(c * CHUNK, CHUNK), CHUNK), :]
        start, stop = (0, pairs) if half is None else (half * pairs // 2, (half + 1) * pairs // 2)
        for j in range(start, stop):
            if j % KEYS == 0:
                with jax.named_scope("wait_k"):
                    kv(k_hbm, kbuf, ksem, c, j, KEYS, KEYS).wait()
                for i in range(j, j + KEYS):
                    refill(c, i)
            with jax.named_scope("scores"):
                both = jnp.concatenate([jnp.where(row == 2 * j, queries, 0.0), jnp.where(row == 2 * j + 1, queries, 0.0)], -1).astype(BF16)
                for t in range(0, cache, TILE):
                    keys = jnp.concatenate([kbuf[slot, 2 * j, t:t + TILE, :], kbuf[slot, 2 * j + 1, t:t + TILE, :]], -1)
                    part = lax.dot_general(both, keys, (((1,), (1,)), ((), ())), preferred_element_type=F32)
                    if j == start:
                        s_v[:, t:t + TILE] = part
                    else:
                        s_v[:, t:t + TILE] += part

        if half is None:
            @pl.when(c == 0)
            def _():
                load(4).wait()
                with jax.named_scope("barrier"):
                    pl.semaphore_wait(barrier, n - 1)

            @pl.when(c >= 2)
            def _():
                finish_h(c - 2)
        elif half == 0:
            finish_h(c - 2)

        with jax.named_scope("softmax"):
            scores = s_v[...] * HEAD**-0.5
            e = jnp.exp(scores - jnp.max(scores, -1, keepdims=True))
            p_v[...] = (e / jnp.sum(e, -1, keepdims=True)).astype(BF16)
        seen = jnp.zeros((CHUNK, HEAD), F32)
        for j in range(start, stop, GROUP):
            with jax.named_scope("wait_v"):
                kv(v_hbm, vbuf, vsem, c, j, GROUP, GROUP).wait()
            for i in range(j, j + GROUP):
                refill(c, pairs + i)
            if half == 1:
                for i in range(5, 9):
                    load(i).start()

            with jax.named_scope("values"):
                values = jnp.concatenate([vbuf[slot, 2 * j + i] for i in range(2 * GROUP)], -1)
                each = jnp.dot(p_v[...], values, preferred_element_type=F32)
                for i in range(2 * GROUP):
                    seen = jnp.where(row == 2 * j + i, each[:, i * HEAD:(i + 1) * HEAD], seen)

        with jax.named_scope("wo"):
            term = jnp.dot(seen.astype(BF16), wo_v[...], preferred_element_type=F32)
            if half is not None:
                c, term = c + half, term[half * HALF:(half + 1) * HALF]
            split(0, c, term, t1)
            scatter(0, c, t1, r1)

    def finish_h(c):
        block = c if whole(c) else blocks - 1
        mine = x_v[pl.ds(pl.multiple_of(block * CHUNK, CHUNK), CHUNK), pl.ds(pl.multiple_of(me * width, width), width)].astype(F32)
        if not whole(c):
            mine = mine[(c - late) * HALF:(c - late + 1) * HALF]
        h = (mine + gathered(0, c, r1)).astype(BF16)
        hown_v[c, :size(c)] = h.astype(F32)
        at(hh, c)[core, chip] = h
        spread(1, c, hh)

    def normed(c):
        with jax.named_scope("wait_h"):
            complete(1, c)
        tiles = [at(hh, c)[k % 2, k // 2].astype(F32) for k in range(n)]
        scale = lax.rsqrt(jnp.sum(sum(wide * wide for wide in tiles), -1, keepdims=True) / d_model + EPS)
        return jnp.concatenate([wide * scale * gm_v[k:k + 1, :].astype(F32) for k, wide in enumerate(tiles)], -1)

    def mlp(*which):
        b = [normed(c) for c in which]
        if sum(size(c) for c in which) % CHUNK:
            b.append(jnp.zeros((HALF, d_model), F32))
        b = jnp.concatenate(b, 0).astype(BF16)
        with jax.named_scope("mlp"):
            gate = jnp.dot(b, wg_v[...], preferred_element_type=F32)
            up = jnp.dot(b, wu_v[...], preferred_element_type=F32)
            hidden = (gate * jax.nn.sigmoid(gate) * up).astype(BF16)
            term = jnp.dot(hidden, wd_v[...], preferred_element_type=F32)
            row = 0
            for c in which:
                split(2, c, term[row:row + size(c)], t2)
                row += size(c)

    def finish_y(c):
        at(yy, c)[core, chip] = (hown_v[c, :size(c)] + gathered(2, c, r2)).astype(BF16)
        spread(3, c, yy)

    def step(c, carry):
        attention(c)
        return carry

    lax.fori_loop(0, blocks - 1, step, 0)
    attention(blocks - 1, 0)
    attention(blocks - 1, 1)

    finish_h(mid)
    finish_h(late)
    with jax.named_scope("wait_w"):
        for i in range(5, 9):
            load(i).wait()
    mlp(*early)
    finish_h(last)
    for c in early:
        scatter(2, c, t2, r2)
    relay(1, mid, hh)
    mlp(mid, late)
    for c in (mid, late):
        scatter(2, c, t2, r2)
    mlp(last)
    scatter(2, last, t2, r2)
    for c in range(chunks):
        finish_y(c)
    for c in range(last):
        relay(3, c, yy)

    for c in (*early, mid):
        with jax.named_scope("wait_y"):
            complete(3, c)
        for k in range(n):
            out_ref[c * CHUNK:(c + 1) * CHUNK, k * width:(k + 1) * width] = at(yy, c)[k % 2, k // 2]
    with jax.named_scope("wait_y"):
        complete(3, late)
        complete(3, last)
    for k in range(n):
        both = [at(yy, c)[k % 2, k // 2].astype(F32) for c in (late, last)]
        out_ref[(blocks - 1) * CHUNK:, k * width:(k + 1) * width] = jnp.concatenate(both, 0).astype(BF16)
    with jax.named_scope("sent"):
        all_sent()


def rotation(place):
    half = HEAD // 2
    angle = np.float64(place) * float(THETA) ** (-np.arange(half) / half)
    cos, sin = np.cos(angle), np.sin(angle)
    table = np.zeros((8, HEAD), np.float32)
    table[0], table[1] = np.concatenate([cos, cos]), np.concatenate([-sin, sin])
    return table


def solution(mesh):
    n = mesh.shape["tp"]

    def step(x, k_cache, v_cache, gain_a, wq, wo, gain_m, w_gate, w_up, w_down):
        rows, d_model = x.shape
        cache = k_cache.shape[1]
        chunks, hidden, width = rows // CHUNK + 1, w_gate.shape[1], d_model // n
        anywhere = pl.BlockSpec(memory_space=pltpu.HBM)
        exchanged = []
        for parts, m in ((chunks - 2, CHUNK), (2, HALF)):
            tiles, arrivals = pltpu.VMEM((parts, 2, n // 2, m, width), BF16), pltpu.VMEM((parts, n - 1, m, width), BF16)
            exchanged += [tiles, arrivals, tiles, tiles, arrivals, tiles, pltpu.VMEM((parts, n // 2, m, width), BF16)]
        dma = pltpu.SemaphoreType.DMA
        return pl.pallas_call(
            functools.partial(kernel, n),
            out_shape=jax.ShapeDtypeStruct((rows, d_model), BF16),
            in_specs=[anywhere] * 11,
            out_specs=pl.BlockSpec(memory_space=pltpu.VMEM),
            scratch_shapes=[
                pltpu.VMEM((SLOTS, CHUNK, cache, HEAD), BF16),
                pltpu.VMEM((SLOTS, CHUNK, cache, HEAD), BF16),
                pltpu.VMEM((rows, d_model), BF16),
                pltpu.VMEM((rows, d_model), BF16),
                pltpu.VMEM((n, width), BF16),
                pltpu.VMEM((n, width), BF16),
                pltpu.VMEM((8, HEAD), F32),
                pltpu.VMEM(wq.shape, BF16),
                pltpu.VMEM(wo.shape, BF16),
                pltpu.VMEM((d_model, hidden), BF16),
                pltpu.VMEM((d_model, hidden), BF16),
                pltpu.VMEM((hidden, d_model), BF16),
                pltpu.VMEM((rows, HEAD), F32),
                pltpu.VMEM((CHUNK, cache), F32),
                pltpu.VMEM((CHUNK, cache), BF16),
                pltpu.VMEM((chunks, 2, n // 2, CHUNK, width), F32),
                pltpu.VMEM((2, chunks, CHUNK, width), F32),
                pltpu.VMEM((chunks, CHUNK, width), F32),
                *exchanged,
                dma((SLOTS, HALF // KEYS)), dma((SLOTS, HALF // GROUP)), dma((9,)), dma(()), dma((4, chunks)), dma((2 * chunks - 1,)),
            ],
            compiler_params=pltpu.CompilerParams(collective_id=0, has_side_effects=True, vmem_limit_bytes=VMEM_LIMIT),
        )(*(pltpu.with_memory_space_constraint(a, pltpu.HBM) for a in (
            x, k_cache.reshape(rows, cache, HEAD), v_cache.reshape(rows, cache, HEAD), gain_a.reshape(n, width), wq, wo,
            gain_m.reshape(n, width), w_gate, w_up, w_down, jnp.asarray(rotation(cache - 1)))))

    states, cache, columns, rows_of = P("dp", None), P("dp", None, "tp", None), P(None, "tp"), P("tp", None)
    return jax.shard_map(
        step,
        mesh=mesh,
        in_specs=(states, cache, cache, P(None), columns, rows_of, P(None), columns, columns, rows_of),
        out_specs=states,
        check_vma=False,
    )
```

time: 50.1 us -> 49.2 us (0.982)
  Pallas kernels: 49.3 us -> 48.5 us
    pallas_call x1, Pallas kernels: 49.3 us -> 48.5 us  [step(): pl.pallas_call(functools.partial(kernel, n), out_shape=jax.ShapeDtypeStru...]
where the time goes in v4:
time: 49.2 us
  Pallas kernels  48.5 us (99%)
  local copies, waits for them, and re-layouts  0.71 us (1%)
    pallas_call x1, Pallas kernels, step(): pl.pallas_call(functools.partial(kernel, n), out_shape=jax.ShapeDtypeStru...  48.5 us

profile of v4, /device:TPU:21, one launch (start us, length us, event | category | flops | bytes accessed | tf_op | source)
XLA Modules:
  0.0 49.2 jit_solution(6273427641978053001)
XLA Ops:
  0.0 48.5 %shard_map.109 = bf16[64,2048]{1,0:T(8,128)(2,1)S(1)} custom-call(bf16[64,2048]{1,0:T(8,128)(2,1)} %x_hbm.1, bf16[64,2048,128]{2,1,0:T(8,128)(2,1)} %bitcast.4, bf16[64,2048,128]{2,1,0:T(8,128)(2,1)} %bitcast.5, bf16[16,128]{1,0:T(8,128)(2,1)} %bitcast.6, bf16[2048,128]{1,0:T(8,128)(2,1)} %wq_hbm.1, bf16[128,2048]{1,0:T(8,128)(2,1)} %wo_hbm.1, ...), custom_call_target="tpu_custom_call" | custom-call | tf_op jit(solution)/shard_map/pallas_call | solution.py:354
  48.5 0.7 %copy.13 = bf16[64,2048]{1,0:T(8,128)(2,1)} copy(bf16[64,2048]{1,0:T(8,128)(2,1)S(1)} %shard_map.109) | data formatting | bytes 524288

commit v5 on v4

--- a/solution.py
+++ b/solution.py
@@ -200,6 +200,9 @@
                     kv(k_hbm, kbuf, ksem, c, j, KEYS, KEYS).wait()
                 for i in range(j, j + KEYS):
                     refill(c, i)
+                if half == 1 and j == start:
+                    for i in range(5, 9):
+                        load(i).start()
             with jax.named_scope("scores"):
                 both = jnp.concatenate([jnp.where(row == 2 * j, queries, 0.0), jnp.where(row == 2 * j + 1, queries, 0.0)], -1).astype(BF16)
                 for t in range(0, cache, TILE):
@@ -233,9 +236,6 @@
                 kv(v_hbm, vbuf, vsem, c, j, GROUP, GROUP).wait()
             for i in range(j, j + GROUP):
                 refill(c, pairs + i)
-            if half == 1:
-                for i in range(5, 9):
-                    load(i).start()
 
             with jax.named_scope("values"):
                 values = jnp.concatenate([vbuf[slot, 2 * j + i] for i in range(2 * GROUP)], -1)

time: 49.2 us -> 49.2 us (level)
  no operation moved by 1% of the time
where the time goes in v5:
time: 49.2 us; the launch traced here: 49.1 us
  Pallas kernels  48.4 us (98%)
  local copies, waits for them, and re-layouts  0.71 us (1%)
    pallas_call x1, Pallas kernels, step(): pl.pallas_call(functools.partial(kernel, n), out_shape=jax.ShapeDtypeStru...  48.4 us

profile of v5, /device:TPU:21, one launch (start us, length us, event | category | flops | bytes accessed | tf_op | source)
XLA Modules:
  0.0 49.1 jit_solution(1499868292291269274)
XLA Ops:
  0.0 48.4 %shard_map.109 = bf16[64,2048]{1,0:T(8,128)(2,1)S(1)} custom-call(bf16[64,2048]{1,0:T(8,128)(2,1)} %x_hbm.1, bf16[64,2048,128]{2,1,0:T(8,128)(2,1)} %bitcast.4, bf16[64,2048,128]{2,1,0:T(8,128)(2,1)} %bitcast.5, bf16[16,128]{1,0:T(8,128)(2,1)} %bitcast.6, bf16[2048,128]{1,0:T(8,128)(2,1)} %wq_hbm.1, bf16[128,2048]{1,0:T(8,128)(2,1)} %wo_hbm.1, ...), custom_call_target="tpu_custom_call" | custom-call | tf_op jit(solution)/shard_map/pallas_call | solution.py:354
  48.4 0.7 %copy.13 = bf16[64,2048]{1,0:T(8,128)(2,1)} copy(bf16[64,2048]{1,0:T(8,128)(2,1)S(1)} %shard_map.109) | data formatting | bytes 524288
